TPU v7x, 32 devices: a whole 2x2x4 slice. The times are simulated.
32 devices in a mesh: date: 4 (over y, x), pix: 8 (over z, core).
Axes of the slice: x: 2, y: 2, z: 4, core: 2. Of those that a mesh axis runs over, the one named last changes fastest.
Arguments:
- stack: bfloat16 [64, 7, 64, 1024], P('date', None, None, 'pix'), may hold values from -8 to 8
- quality: int32 [64, 64, 1024], P('date', None, 'pix'), may hold values from 0 to 1073741823
- days: int32 [64], P('date'), may hold values from 8 to 1536, as said below
Outputs:
- coef: float32 [7, 8, 64, 1024], P(None, None, 'pix', 'date')
- score: float32 [7, 64, 1024], P(None, 'pix', 'date')
Inputs may be any that keep to these rules, and one draw needn't show every extreme that they name: `days`: strictly increasing.
All inputs are finite; a program needn't handle non-finite values.
Results may differ from a plain program's by a relative error of at most 0.0003.
Values may be sent and summed in bfloat16 or wider, within the bound.
A program may use at most 256 MiB of HBM per device.

v0:
```python
import jax
import jax.numpy as jnp
from jax import lax
from jax.sharding import PartitionSpec as P

RIDGE_TERM = 1.0
PAIR_LIST = [(first, second) for first in range(8) for second in range(first, 8)]


def pair_number(first, second):
    return PAIR_LIST.index((min(first, second), max(first, second)))


def design_matrix(days):
    moment_t = days.astype(jnp.float32)
    columns = [jnp.ones_like(moment_t), (moment_t - 512.0) / 512.0]
    for order in range(1, 4):
        phase = 2.0 * jnp.pi * order * moment_t / 365.25
        columns.append(jnp.cos(phase))
        columns.append(jnp.sin(phase))
    return jnp.stack(columns, 1)


def weights(quality):
    cloud = jnp.bitwise_and(jnp.right_shift(quality, 3), 1)
    level = jnp.bitwise_and(jnp.right_shift(quality, 8), 3)
    return (1 - cloud).astype(jnp.float32) / (1.0 + level.astype(jnp.float32))


def pair_products(design):
    return jnp.stack([design[:, first] * design[:, second] for first, second in PAIR_LIST], 1)


def chol_solve(gram, moment):
    lower = {}
    for first in range(8):
        for second in range(first + 1):
            total = gram[pair_number(first, second)]
            if first == second:
                total = total + RIDGE_TERM
            for inner in range(second):
                total = total - lower[first, inner] * lower[second, inner]
            if first == second:
                lower[first, first] = jnp.sqrt(total)
            else:
                lower[first, second] = total / lower[second, second]
    forward = []
    for first in range(8):
        total = moment[first]
        for inner in range(first):
            total = total - lower[first, inner][None, :] * forward[inner]
        forward.append(total / lower[first, first][None, :])
    backward = [None] * 8
    for first in range(7, -1, -1):
        total = forward[first]
        for inner in range(first + 1, 8):
            total = total - lower[inner, first][None, :] * backward[inner]
        backward[first] = total / lower[first, first][None, :]
    return jnp.stack(backward, 0)


def local(stack, quality, days):
    high = lax.Precision.HIGHEST
    bands = stack.shape[1]
    local_dates, all_rows, arrive_cols = (stack.shape[0], stack.shape[2], stack.shape[3])
    arrive_pixels = all_rows * arrive_cols
    design = design_matrix(days)
    weight = weights(quality).reshape(local_dates, arrive_pixels)
    samples = stack.reshape(local_dates, bands, arrive_pixels).astype(jnp.float32)
    gram_part = jnp.dot(pair_products(design).T, weight, precision=high)
    weighted = weight[:, None, :] * samples
    moment_part = jnp.dot(
        design.T, weighted.reshape(local_dates, bands * arrive_pixels), precision=high
    )
    square_part = jnp.sum(weighted * samples, 0)
    weight_part = jnp.sum(weight, 0)[None, :]
    stacked = jnp.concatenate(
        [gram_part, moment_part.reshape(8 * bands, arrive_pixels), square_part, weight_part], 0
    )
    stacked = stacked.reshape(stacked.shape[0], all_rows, arrive_cols)
    spread = lax.all_to_all(stacked, "pix", split_axis=1, concat_axis=2, tiled=True)
    summed = lax.psum_scatter(spread, "date", scatter_dimension=2, tiled=True)
    row_count, col_count = (summed.shape[1], summed.shape[2])
    pixels = row_count * col_count
    summed = summed.reshape(summed.shape[0], pixels)
    gram = summed[:36]
    moment = summed[36 : 36 + 8 * bands].reshape(8, bands, pixels)
    squares = summed[36 + 8 * bands : 36 + 9 * bands]
    wsum = summed[36 + 9 * bands]
    coef_flat = chol_solve(gram, moment)
    ssr = squares - 2.0 * jnp.sum(coef_flat * moment, 0)
    for first in range(8):
        for second in range(8):
            ssr = (
                ssr
                + gram[pair_number(first, second)][None, :] * coef_flat[first] * coef_flat[second]
            )
    total_ssr, total_weight = lax.psum((jnp.sum(ssr, 1), jnp.sum(wsum)), ("date", "pix"))
    sigma2 = total_ssr / total_weight
    score = jnp.sqrt(ssr / (wsum[None, :] + 1.0)) / jnp.sqrt(sigma2)[:, None]
    coef = jnp.transpose(coef_flat.reshape(8, bands, row_count, col_count), (1, 0, 2, 3))
    return (coef, score.reshape(bands, row_count, col_count))


def solution(mesh):
    return jax.shard_map(
        local,
        mesh=mesh,
        in_specs=(P("date", None, None, "pix"), P("date", None, "pix"), P("date")),
        out_specs=(P(None, None, "pix", "date"), P(None, "pix", "date")),
        check_vma=False,
    )
```

profile of v0, /device:TPU:0, one launch (start us, length us, event | category | flops | bytes accessed | tf_op | source)
XLA Modules:
  0.0 227.7 jit_solution(3004523274341131072)
XLA Ops:
  7.2 1.2 fusion.103
  8.5 2.0 fusion
  11.3 0.3 copy.246
  11.6 0.4 mul.6375
  12.0 3.9 %copy.189 = f32[2,8,7,8192]{3,1,2,0:T(8,128)} copy(f32[2,8,7,8192]{3,2,1,0:T(8,128)S(1)} %bitcast.504) | data formatting | bytes 7340032
  15.9 2.2 convert.1
  18.2 8.7 %fusion.1 = f32[8,57344]{1,0:T(8,128)} fusion(f32[16,8]{1,0:T(8,128)S(1)} %stack.167, f32[16,57344]{1,0:T(8,128)} %bitcast.505, f32[2,8,448,128]{3,2,1,0:T(8,128)} %convert.1), kind=kOutput, calls=%fused_computation.3 | convolution fusion | flops 88997888 | bytes 9175552 | tf_op jit(solution)/shard_map/dot_general | solution.py:72
  26.9 1.8 concatenate.9
  28.7 2.3 %copy.183 = f32[56,64,128]{2,0,1:T(8,128)} copy(f32[56,64,128]{2,1,0:T(8,128)S(1)} %concatenate.9) | data formatting | bytes 3670016 | tf_op jit(solution)/shard_map/concatenate | solution.py:77
  33.5 1.2 fusion.3
  34.8 0.3 pad_maximum_fusion
  35.1 83.3 %all_to_all.18 = f32[100,64,128]{2,0,1:T(8,128)S(1)} all-to-all(f32[100,64,128]{2,0,1:T(8,128)S(1)} %pad_maximum_fusion), channel_id=1, replica_groups=mesh['date'=4,'pix'=8] {'pix'}, dimensions={1} | all-to-all | bytes 6553600 | tf_op jit(solution)/shard_map/all_to_all | solution.py:81
  118.4 2.3 copy.245
  120.7 44.1 %reduce-scatter.2.cloned.1.call-done = f32[100,8,256]{2,1,0:T(8,128)} async-done(((f32[100,8,1024]{2,1,0:T(8,128)}), f32[100,8,256]{2,1,0:T(8,128)}) %reduce-scatter.2.cloned.1.call-update) | async-done | bytes 819216 | tf_op jit(solution)/shard_map/reduce_scatter | solution.py:82
  164.8 0.9 add_bitcast_fusion
  165.7 1.5 slice_reduce_fusion
  167.6 0.9 fusion.104
  168.6 0.8 rsqrt_multiply_fusion.39
  169.4 0.9 rsqrt_multiply_fusion.28
  170.3 0.9 rsqrt_multiply_fusion.26
  171.1 0.9 rsqrt_multiply_fusion.27
  172.0 0.7 rsqrt_multiply_fusion.40
  172.7 0.8 rsqrt_multiply_fusion.18
  173.5 0.8 subtract_sqrt_fusion.7
  174.3 0.8 rsqrt_multiply_fusion.10
  175.1 0.8 subtract_sqrt_fusion.6
  176.7 0.4 divide_dynamic-update-slice_fusion
  178.0 0.9 fusion.93
  179.2 0.8 copy.186
  180.0 39.5 %all-reduce = (f32[7]{0:T(128)S(1)}, f32[]{:T(128)}) all-reduce(f32[7]{0:T(128)S(1)} %get-tuple-element.12, f32[]{:T(128)} %get-tuple-element.192), channel_id=1, replica_groups=mesh['date'=4,'pix'=8] {'date','pix'}, use_global_device_ids=true, to_apply=%region_5.0 | all-reduce | flops 8 | bytes 64 | tf_op jit(solution)/shard_map/psum | solution.py:98
  219.5 0.7 divide_sqrt_fusion
  220.2 0.7 sqrt_divide_fusion
  (130 shorter events, 5.3 us)
Async XLA Ops:
  7.2 3.5 %copy-start.3 = (s32[16]{0:T(128)S(1)}, s32[16]{0:T(128)}, u32[]{:S(2)}) copy-start(s32[16]{0:T(128)} %param.5) | copy-start | bytes 196
  7.2 157.6 %reduce-scatter.2.cloned.1.call-start = ((), (), s32[]{:S(2)}) async-start(), calls=%async_computation.2 | async-start | bytes 4096000 | tf_op jit(solution)/shard_map/reduce_scatter | solution.py:82
  12.0 3.9 %copy-start.1 = (bf16[16,7,64,128]{3,2,1,0:T(8,128)(2,1)S(1)}, bf16[16,7,64,128]{3,2,1,0:T(8,128)(2,1)}, u32[]{:S(2)}) copy-start(bf16[16,7,64,128]{3,2,1,0:T(8,128)(2,1)} %param.3) | copy-start | bytes 5505028
  31.0 3.7 %copy-start.2 = (f32[56,64,128]{2,0,1:T(8,128)S(1)}, f32[56,64,128]{2,0,1:T(8,128)}, u32[]{:S(2)}) copy-start(f32[56,64,128]{2,0,1:T(8,128)} %copy.183) | copy-start | bytes 5505028
  164.8 11.1 %copy-start = (f32[100,8,256]{2,1,0:T(8,128)S(1)}, f32[100,8,256]{2,1,0:T(8,128)}, u32[]{:S(2)}) copy-start(f32[100,8,256]{2,1,0:T(8,128)} %reduce-scatter.2.cloned.1.call-done) | copy-start | bytes 2457604
  176.3 1.4 slice-start
Sparse Core Ops, SparseCore 0:
  120.8 43.9 reduce-scatter.1
where the time goes:
time: 229 us; the launch traced here: 228 us
  blocking collectives  123 us (54%)
  waiting for transfers between devices  44.1 us (19%)
  other arithmetic  19.6 us (9%)
  local copies, waits for them, and re-layouts  16.5 us (7%)
  between operations  14.7 us (6%)
  matrix products  9.93 us (4%)
    all_to_all x1, blocking collectives, local(): lax.all_to_all(stacked, 'pix', split_axis=1, concat_axis=2, tiled=True)  83.3 us
    reduce_scatter x1, waiting for transfers between devices, local(): summed = lax.psum_scatter(spread, 'date', scatter_dimension=2, tiled=True)  44.1 us
    psum x1, blocking collectives, local(): lax.psum((jnp.sum(ssr, 1), jnp.sum(wsum)), ('date', 'pix'))  39.5 us
    dot_general x1, matrix products, local(): jnp.dot(design.T, weighted.reshape(local_dates, bands * arrive_pixels), p...  8.69 us
    div x14, other arithmetic, chol_solve(): lower[first, second] = total / lower[second, second]  5.87 us
    unnamed x54, local copies, waits for them, and re-layouts  5.3 us
  transfers between devices with their start and end apart: 1, of which 1 were waited for; matrix products, arithmetic and copies ran while one was open for 0% of the time, Pallas kernels for 0%

commit v1 on v0

--- a/solution.py
+++ b/solution.py
@@ -95,7 +95,7 @@
                 ssr
                 + gram[pair_number(first, second)][None, :] * coef_flat[first] * coef_flat[second]
             )
-    total_ssr, total_weight = lax.psum((jnp.sum(ssr, 1), jnp.sum(wsum)), ("date", "pix"))
+    total_ssr, total_weight = lax.psum(lax.psum((jnp.sum(ssr, 1), jnp.sum(wsum)), "date"), "pix")
     sigma2 = total_ssr / total_weight
     score = jnp.sqrt(ssr / (wsum[None, :] + 1.0)) / jnp.sqrt(sigma2)[:, None]
     coef = jnp.transpose(coef_flat.reshape(8, bands, row_count, col_count), (1, 0, 2, 3))

time: 229 us -> 214 us (0.934)
  blocking collectives: 123 us -> 108 us
    psum x1 -> x2, blocking collectives: 39.5 us -> 24.3 us  [the longest x1 14.8 us: local(): lax.psum(lax.psum((jnp.sum(ssr, 1), jnp.sum(wsum)), 'date'), 'pix')]
where the time goes in v1:
time: 214 us; the launch traced here: 213 us
  blocking collectives  108 us (50%)
  waiting for transfers between devices  44.1 us (21%)
  other arithmetic  19.6 us (9%)
  local copies, waits for them, and re-layouts  16.5 us (8%)
  between operations  14.7 us (7%)
  matrix products  9.93 us (5%)
    all_to_all x1, blocking collectives, local(): lax.all_to_all(stacked, 'pix', split_axis=1, concat_axis=2, tiled=True)  83.3 us
    reduce_scatter x1, waiting for transfers between devices, local(): summed = lax.psum_scatter(spread, 'date', scatter_dimension=2, tiled=True)  44.1 us
    psum x1, blocking collectives, local(): lax.psum(lax.psum((jnp.sum(ssr, 1), jnp.sum(wsum)), 'date'), 'pix')  14.8 us
    psum x1, blocking collectives, local(): lax.psum((jnp.sum(ssr, 1), jnp.sum(wsum)), 'date')  9.54 us
    dot_general x1, matrix products, local(): jnp.dot(design.T, weighted.reshape(local_dates, bands * arrive_pixels), p...  8.69 us
    div x14, other arithmetic, chol_solve(): lower[first, second] = total / lower[second, second]  5.87 us
    unnamed x54, local copies, waits for them, and re-layouts  5.31 us
  transfers between devices with their start and end apart: 1, of which 1 were waited for; matrix products, arithmetic and copies ran while one was open for 0% of the time, Pallas kernels for 0%

profile of v1, /device:TPU:0, one launch (start us, length us, event | category | flops | bytes accessed | tf_op | source)
XLA Modules:
  0.0 212.5 jit_solution(11609800216391630051)
XLA Ops:
  7.2 1.2 fusion.103
  8.5 2.0 fusion
  11.6 0.4 mul.6375
  12.0 3.9 %copy.189 = f32[2,8,7,8192]{3,1,2,0:T(8,128)} copy(f32[2,8,7,8192]{3,2,1,0:T(8,128)S(1)} %bitcast.504) | data formatting | bytes 7340032
  16.0 2.2 %convert.1 = f32[2,8,448,128]{3,2,1,0:T(8,128)} convert(bf16[2,8,448,128]{3,2,1,0:T(8,128)(2,1)S(1)} %bitcast.508) | non-fusion elementwise | flops 917504 | bytes 5505024
  18.3 8.7 %fusion.1 = f32[8,57344]{1,0:T(8,128)} fusion(f32[16,8]{1,0:T(8,128)S(1)} %stack.167, f32[16,57344]{1,0:T(8,128)} %bitcast.505, f32[2,8,448,128]{3,2,1,0:T(8,128)} %convert.1), kind=kOutput, calls=%fused_computation.3 | convolution fusion | flops 88997888 | bytes 9175552 | tf_op jit(solution)/shard_map/dot_general | solution.py:72
  26.9 1.8 concatenate.9
  28.7 2.3 %copy.183 = f32[56,64,128]{2,0,1:T(8,128)} copy(f32[56,64,128]{2,1,0:T(8,128)S(1)} %concatenate.9) | data formatting | bytes 3670016 | tf_op jit(solution)/shard_map/concatenate | solution.py:77
  33.5 1.2 fusion.3
  34.8 0.3 pad_maximum_fusion
  35.1 83.3 %all_to_all.18 = f32[100,64,128]{2,0,1:T(8,128)S(1)} all-to-all(f32[100,64,128]{2,0,1:T(8,128)S(1)} %pad_maximum_fusion), channel_id=1, replica_groups=mesh['date'=4,'pix'=8] {'pix'}, dimensions={1} | all-to-all | bytes 6553600 | tf_op jit(solution)/shard_map/all_to_all | solution.py:81
  118.4 2.3 %copy.245 = f32[100,8,8,128]{3,1,2,0:T(8,128)} copy(f32[100,8,8,128]{3,0,1,2:T(8,128)S(1)} %bitcast.506) | data formatting | bytes 6553600 | tf_op jit(solution)/shard_map/all_to_all | solution.py:81
  120.7 44.1 %reduce-scatter.2.cloned.1.call-done = f32[100,8,256]{2,1,0:T(8,128)} async-done(((f32[100,8,1024]{2,1,0:T(8,128)}), f32[100,8,256]{2,1,0:T(8,128)}) %reduce-scatter.2.cloned.1.call-update) | async-done | bytes 819216 | tf_op jit(solution)/shard_map/reduce_scatter | solution.py:82
  164.8 0.9 add_bitcast_fusion
  165.7 1.5 slice_reduce_fusion
  167.6 0.9 fusion.104
  168.6 0.8 rsqrt_multiply_fusion.39
  169.4 0.9 rsqrt_multiply_fusion.28
  170.3 0.9 rsqrt_multiply_fusion.26
  171.1 0.9 rsqrt_multiply_fusion.27
  172.0 0.7 rsqrt_multiply_fusion.40
  172.7 0.8 rsqrt_multiply_fusion.18
  173.5 0.8 subtract_sqrt_fusion.7
  174.3 0.8 rsqrt_multiply_fusion.10
  175.1 0.8 subtract_sqrt_fusion.6
  176.7 0.4 divide_dynamic-update-slice_fusion
  178.0 0.9 fusion.93
  179.2 0.8 copy.186
  180.0 9.5 %all-reduce.1 = (f32[7]{0:T(128)S(1)}, f32[]{:T(128)}) all-reduce(f32[7]{0:T(128)S(1)} %get-tuple-element.14, f32[]{:T(128)} %get-tuple-element.194), channel_id=1, replica_groups=mesh['date'=4,'pix'=8] {'date'}, use_global_device_ids=true, to_apply=%region_5.0 | all-reduce | flops 8 | bytes 64 | tf_op jit(solution)/shard_map/psum | solution.py:98
  189.5 14.8 %all-reduce = (f32[7]{0:T(128)S(1)}, f32[]{:T(128)}) all-reduce(f32[7]{0:T(128)S(1)} %get-tuple-element.12, f32[]{:T(128)} %get-tuple-element.13), channel_id=1, replica_groups=mesh['date'=4,'pix'=8] {'pix'}, use_global_device_ids=true, to_apply=%region_6.0 | all-reduce | flops 8 | bytes 64 | tf_op jit(solution)/shard_map/psum | solution.py:98
  204.3 0.7 divide_sqrt_fusion
  205.0 0.7 sqrt_divide_fusion
  (131 shorter events, 5.6 us)
Async XLA Ops:
  7.2 3.5 %copy-start.3 = (s32[16]{0:T(128)S(1)}, s32[16]{0:T(128)}, u32[]{:S(2)}) copy-start(s32[16]{0:T(128)} %param.5) | copy-start | bytes 196
  7.2 157.6 %reduce-scatter.2.cloned.1.call-start = ((), (), s32[]{:S(2)}) async-start(), calls=%async_computation.2 | async-start | bytes 4096000 | tf_op jit(solution)/shard_map/reduce_scatter | solution.py:82
  12.0 3.9 %copy-start.1 = (bf16[16,7,64,128]{3,2,1,0:T(8,128)(2,1)S(1)}, bf16[16,7,64,128]{3,2,1,0:T(8,128)(2,1)}, u32[]{:S(2)}) copy-start(bf16[16,7,64,128]{3,2,1,0:T(8,128)(2,1)} %param.3) | copy-start | bytes 5505028
  31.0 3.7 %copy-start.2 = (f32[56,64,128]{2,0,1:T(8,128)S(1)}, f32[56,64,128]{2,0,1:T(8,128)}, u32[]{:S(2)}) copy-start(f32[56,64,128]{2,0,1:T(8,128)} %copy.183) | copy-start | bytes 5505028
  164.8 11.1 %copy-start = (f32[100,8,256]{2,1,0:T(8,128)S(1)}, f32[100,8,256]{2,1,0:T(8,128)}, u32[]{:S(2)}) copy-start(f32[100,8,256]{2,1,0:T(8,128)} %reduce-scatter.2.cloned.1.call-done) | copy-start | bytes 2457604
  176.3 1.4 slice-start
Sparse Core Ops, SparseCore 0:
  120.8 43.9 reduce-scatter.1
